TPU v7x, 32 devices: a whole 2x2x4 slice. The times are simulated.
32 devices in a mesh: grp: 2 (over x), row: 16 (over z, y, core).
Axes of the slice: x: 2, y: 2, z: 4, core: 2. Of those that a mesh axis runs over, the one named last changes fastest.
Arguments:
- tiles: bfloat16 [192, 512, 512], P(('grp', 'row')), may hold values from -0.15625 to 0.15625
- tile_row: int32 [192], P(('grp', 'row')), may hold values from 0 to 63, as said below
- tile_col: int32 [192], P(('grp', 'row')), may hold values from 0 to 63, as said below
- tile_count: int32 [32], P(('grp', 'row')), may hold values from 3 to 6, as said below
- q_block: bfloat16 [32768, 256], P(('grp', 'row')), may hold values from -80 to 80
Outputs:
- q_next: float32 [32768, 256], P(('grp', 'row'))
Inputs may be any that keep to these rules, and one draw needn't show every extreme that they name: `tile_row`: each slot names one of its device's tile rows: d * 2 to d * 2 + 1 for device d. `tile_col`: each slot's tile column is (tile_row + o) mod 64 with o from minus 2 to 2; no two slots of one device name the same pair of tile row and tile column. `tile_count`: some device has all 6 slots live.
All inputs are finite; a program needn't handle non-finite values.
Results may differ from a plain program's by a relative error of at most 0.0029.
Values may be sent and summed in bfloat16 or wider, within the bound.
A program may use at most 64 MiB of HBM per device.

v0:
```python
import jax
import jax.numpy as jnp
from jax import lax
from jax.sharding import PartitionSpec as P

H = 2


def padded_2(block, sides, width):
    for axis, dim in sides:
        count = lax.axis_size(axis)
        forward = [(i, i + 1) for i in range(count - 1)]
        forward.append((count - 1, 0))
        backward = [(target, source) for source, target in forward]
        low = lax.ppermute(
            lax.slice_in_dim(block, block.shape[dim] - width, None, axis=dim), axis, forward
        )
        high = lax.ppermute(lax.slice_in_dim(block, 0, width, axis=dim), axis, backward)
        block = jnp.concatenate([low, block, high], axis=dim)
    return block


def passed_along(block, axis, distance):
    devices = range(lax.axis_size(axis))
    route = [((i - distance) % len(devices), i) for i in devices]
    return lax.ppermute(block, axis, route)


def on_device(tiles, tile_row, tile_col, tile_count, q_block):
    slot_count, tile_size, unused_size = tiles.shape
    basis_width = q_block.shape[1]
    own_tiles = q_block.shape[0] // tile_size
    window = own_tiles + 2 * H
    tile_total = own_tiles * lax.axis_size("grp") * lax.axis_size("row")
    local_row = tile_row % own_tiles
    local_col = (tile_col - tile_row + H) % tile_total + local_row
    padded = padded_2(q_block, ((("grp", "row"), 0),), H * tile_size)
    stack = padded.reshape(window, tile_size, basis_width)
    live_slot = jnp.arange(slot_count, dtype=jnp.int32) < tile_count[0]
    blocks = stack[local_col]
    blocks = jnp.where(live_slot[:, None, None], blocks, jnp.zeros_like(blocks))
    products = jnp.einsum("sab,sbk->sak", tiles, blocks, preferred_element_type=jnp.float32)
    row_ids = jnp.arange(own_tiles, dtype=jnp.int32)
    row_place = ((local_row[None, :] == row_ids[:, None]) & live_slot[None, :]).astype(jnp.float32)
    aq_tiles = jnp.einsum(
        "rs,sak->rak", row_place, products, precision=lax.Precision.HIGHEST
    ).astype(jnp.bfloat16)
    row_part = aq_tiles[local_row]
    images = jnp.einsum("sab,sak->sbk", tiles, row_part, preferred_element_type=jnp.float32)
    column_ids = jnp.arange(window, dtype=jnp.int32)
    col_place = ((local_col[None, :] == column_ids[:, None]) & live_slot[None, :]).astype(
        jnp.float32
    )
    sums = jnp.einsum("cs,sbk->cbk", col_place, images, precision=lax.Precision.HIGHEST)
    own_part = sums[H : H + own_tiles]
    lower = sums[:H].astype(jnp.bfloat16).reshape(H * tile_size, basis_width)
    upper = sums[H + own_tiles :].astype(jnp.bfloat16).reshape(H * tile_size, basis_width)
    from_below = passed_along(upper, ("grp", "row"), 1)
    from_above = passed_along(lower, ("grp", "row"), -1)
    below_tiles = from_below.astype(jnp.float32).reshape(H, tile_size, basis_width)
    above_tiles = from_above.astype(jnp.float32).reshape(H, tile_size, basis_width)
    own_part = own_part + below_tiles
    own_part = own_part + above_tiles
    local_y = own_part.reshape(own_tiles * tile_size, basis_width)
    rows_total = tile_total * tile_size
    local_gram = jnp.dot(
        local_y.T, local_y, precision=lax.Precision.HIGHEST, preferred_element_type=jnp.float32
    )
    gram_matrix = lax.psum(local_gram, ("grp", "row")) / rows_total
    factor_low = jnp.linalg.cholesky(gram_matrix)
    return lax.linalg.triangular_solve(
        factor_low, local_y, left_side=False, lower=True, transpose_a=True
    )


def solution(mesh):
    placed = (
        P(("grp", "row"), None, None),
        P(("grp", "row")),
        P(("grp", "row")),
        P(("grp", "row")),
        P(("grp", "row"), None),
    )
    return jax.shard_map(
        on_device, mesh=mesh, in_specs=placed, out_specs=P(("grp", "row"), None), check_vma=False
    )
```

profile of v0, /device:TPU:0, one launch (start us, length us, event | category | flops | bytes accessed | tf_op | source)
XLA Modules:
  0.0 289.4 jit_solution(1188874127921917125)
XLA Ops:
  6.5 0.5 collective-permute-start
  7.0 5.9 %collective-permute-start.1 = (bf16[1024,256]{1,0:T(8,128)(2,1)}, bf16[1024,256]{1,0:T(8,128)(2,1)S(1)}, u32[]{:S(2)}, u32[]{:S(2)}) collective-permute-start(bf16[1024,256]{1,0:T(8,128)(2,1)} %param.9), channel_id=1, source_target_pairs={{1,0},{2,1},{3,2},{4,3},{5,4},{6,5},{7,6},{8,7},{9,8},{10,9},{11,1... | collective-permute-start | bytes 1572872 | tf_op jit(solution)/shard_map/ppermute | solution.py:18
  12.9 0.7 compare_select_fusion
  14.3 0.7 compare_select_fusion.1
  15.0 5.1 %collective-permute-done = bf16[1024,256]{1,0:T(8,128)(2,1)S(1)} collective-permute-done((bf16[1024,256]{1,0:T(8,128)(2,1)}, bf16[1024,256]{1,0:T(8,128)(2,1)S(1)}, u32[]{:S(2)}, u32[]{:S(2)}) %collective-permute-start) | collective-permute-done | bytes 524320 | tf_op jit(solution)/shard_map/ppermute | solution.py:15
  20.1 2.3 pad_maximum_fusion
  22.4 3.3 %gather_fusion = bf16[6,512,256]{2,1,0:T(8,128)(2,1)} fusion(bf16[6,512,256]{2,1,0:T(8,128)(2,1)} %bitcast.63, s32[1024]{0:T(1024)S(1)} %pad_clamp_fusion.1), kind=kCustom, calls=%fused_computation | custom fusion | bytes 3145752 | tf_op jit(solution)/shard_map/gather | solution.py:40
  25.7 4.3 %convolution_bitcast_fusion.1 = f32[6,512,256]{1,2,0:T(8,128)} fusion(bf16[6,512,512]{2,1,0:T(8,128)(2,1)S(1)} %copy-done, bf16[6,512,256]{2,1,0:T(8,128)(2,1)} %gather_fusion, pred[6]{0:T(512)(128)(4,1)S(1)} %iota_compare_fusion.4), kind=kOutput, calls=%fused_computation.5 | convolution fusion | flops 806092800 | bytes 7864326 | tf_op jit(solution)/shard_map/sab,sbk->sak/dot_general | solution.py:42
  29.9 5.1 %copy.32 = f32[6,512,256]{2,0,1:T(8,128)} copy(f32[6,512,256]{1,2,0:T(8,128)} %convolution_bitcast_fusion.1) | data formatting | bytes 6291456 | tf_op jit(solution)/shard_map/sab,sbk->sak/dot_general | solution.py:42
  35.1 4.3 %convolution_convert_fusion = bf16[2,512,256]{2,0,1:T(2,128)(2,1)S(1)} fusion(f32[6,512,256]{2,0,1:T(8,128)} %copy.32, pred[6]{0:T(512)(128)(4,1)S(1)} %iota_compare_fusion.4, s32[6]{0:T(128)S(1)} %get-tuple-element.22), kind=kOutput, calls=%fused_computation.9 | convolution fusion | flops 19136536 | bytes 3670046 | tf_op jit(solution)/shard_map/rs,sak->rak/dot_general | solution.py:45
  39.4 0.9 copy.33
  40.2 2.9 gather_fusion.1
  43.1 4.1 %convolution_bitcast_fusion = f32[6,512,256]{1,2,0:T(8,128)} fusion(bf16[6,512,256]{2,1,0:T(8,128)(2,1)} %gather_fusion.1, bf16[6,512,512]{2,1,0:T(8,128)(2,1)S(1)} %copy-done), kind=kOutput, calls=%fused_computation.4 | convolution fusion | flops 805306368 | bytes 7864320 | tf_op jit(solution)/shard_map/sab,sak->sbk/dot_general | solution.py:49
  47.2 5.1 %copy.35 = f32[6,512,256]{2,0,1:T(8,128)} copy(f32[6,512,256]{1,2,0:T(8,128)} %convolution_bitcast_fusion) | data formatting | bytes 6291456 | tf_op jit(solution)/shard_map/sab,sak->sbk/dot_general | solution.py:49
  52.3 4.3 %fusion.32 = (bf16[6,512,256]{2,0,1:T(8,128)(2,1)S(1)}, f32[6,512,256]{2,0,1:T(8,128)S(1)}) fusion(f32[6,512,256]{2,0,1:T(8,128)} %copy.35, s32[6]{0:T(128)S(1)} %get-tuple-element.24, pred[6]{0:T(512)(128)(4,1)S(1)} %iota_compare_fusion.4), kind=kOutput, calls=%fused_computation.71 | convolution fusion | flops 57409608 | bytes 7864350 | tf_op jit(solution)/shard_map/cs,sbk->cbk/dot_general | solution.py:54
  56.6 0.7 fusion.31
  57.4 0.1 copy.37
  57.5 4.0 %collective-permute-start.2 = (bf16[1024,256]{1,0:T(8,128)(2,1)S(1)}, bf16[1024,256]{1,0:T(8,128)(2,1)S(1)}, u32[]{:S(2)}, u32[]{:S(2)}) collective-permute-start(bf16[1024,256]{1,0:T(8,128)(2,1)S(1)} %bitcast.64), channel_id=1, source_target_pairs={{31,0},{0,1},{1,2},{2,3},{3,4},{4,5},{5,6},{6,7},{7,8},{8,9},{9,10... | collective-permute-start | bytes 1572872 | tf_op jit(solution)/shard_map/ppermute | solution.py:26
  61.5 0.1 copy.38
  61.6 1.6 collective-permute-start.3
  63.2 0.5 slice.71
  63.7 6.1 %collective-permute-done.2 = bf16[1024,256]{1,0:T(8,128)(2,1)S(1)} collective-permute-done((bf16[1024,256]{1,0:T(8,128)(2,1)S(1)}, bf16[1024,256]{1,0:T(8,128)(2,1)S(1)}, u32[]{:S(2)}, u32[]{:S(2)}) %collective-permute-start.2) | collective-permute-done | bytes 524320 | tf_op jit(solution)/shard_map/ppermute | solution.py:26
  69.9 0.1 fusion.2
  70.0 1.0 copy-done.1
  71.0 2.5 convolution_bitcast_fusion.2
  73.6 132.1 %all-reduce.3.cloned.1.call-done = f32[256,256]{0,1:T(8,128)} async-done(((f32[256,256]{0,1:T(8,128)}), f32[256,256]{0,1:T(8,128)}) %all-reduce.3.cloned.1.call-update) | async-done | bytes 262160 | tf_op jit(solution)/shard_map/psum | solution.py:69
  205.6 1.7 broadcast_multiply_fusion
  207.3 1.1 copy.41
  208.4 1.0 fusion.7
  209.4 0.7 copy-done.3
  210.1 11.7 %cholesky.50 = f32[128,128]{1,0:T(8,128)S(1)} custom-call(f32[128,128]{1,0:T(8,128)S(1)} %cholesky.118), custom_call_target="Cholesky" | custom-call | tf_op jit(solution)/shard_map/jit(cholesky)/cholesky | solution.py:70
  221.9 9.8 %custom-call.14 = f32[1,128,128]{1,2,0:T(8,128)S(1)} custom-call(f32[1,128,128]{2,1,0:T(8,128)S(1)} %get-tuple-element.32), custom_call_target="InvertDiagBlocksLowerTriangular" | custom-call | tf_op jit(solution)/shard_map/jit(cholesky)/cholesky | solution.py:70
  231.7 1.0 constant_dynamic-update-slice_fusion.1
  232.7 1.1 convolution_subtract_fusion
  233.8 11.9 %cholesky.105 = f32[128,128]{1,0:T(8,128)S(1)} custom-call(f32[128,128]{1,0:T(8,128)S(1)} %convolution_subtract_fusion), custom_call_target="Cholesky" | custom-call | tf_op jit(solution)/shard_map/jit(cholesky)/cholesky | solution.py:70
  245.8 0.7 compare_reduce_fusion
  247.8 1.0 select_select_fusion
  248.8 5.3 %while.1 = (s32[]{:T(128)}, f32[256,256]{1,0:T(8,128)S(1)}, s32[2,2]{1,0:T(2,128)S(1)}, f32[2,128,128]{2,1,0:T(8,128)}, s32[]{:T(128)}) while((s32[]{:T(128)}, f32[256,256]{1,0:T(8,128)S(1)}, s32[2,2]{1,0:T(2,128)S(1)}, f32[2,128,128]{2,1,0:T(8,128)}, s32[]{:T(128)}) %tuple.27), condition=%wide.while_cond, body=%wide.while_body.sunk | while | flops 2 | bytes 132705 | solution.py:71
  248.8 0.7 fusion.44
  249.5 2.0 bitcast_dynamic-update-slice_fusion.2
  251.5 0.7 fusion.44
  252.2 2.0 bitcast_dynamic-update-slice_fusion.2
  254.1 20.5 %custom-call.15 = f32[2,128,128]{1,2,0:T(8,128)S(1)} custom-call(f32[2,128,128]{2,1,0:T(8,128)} %get-tuple-element.12), custom_call_target="InvertDiagBlocksLowerTriangular" | custom-call | tf_op jit(solution)/shard_map/triangular_solve | solution.py:71
  274.6 1.7 fusion.5
  276.3 1.0 fusion.8
  277.3 1.7 fusion.4
  279.0 1.0 pad_maximum_fusion.1
  280.0 2.5 copy.42
  (22 shorter events, 0.3 us)
Async XLA Ops:
  6.5 19.2 %copy-start = (bf16[6,512,512]{2,1,0:T(8,128)(2,1)S(1)}, bf16[6,512,512]{2,1,0:T(8,128)(2,1)}, u32[]{:S(2)}) copy-start(bf16[6,512,512]{2,1,0:T(8,128)(2,1)} %param.5) | copy-start | bytes 9437188
  6.5 199.1 %all-reduce.3.cloned.1.call-start = ((), (), s32[]{:S(2)}) async-start(), calls=%async_computation | async-start | bytes 524288 | tf_op jit(solution)/shard_map/psum | solution.py:69
  6.5 13.6 %collective-permute-start = (bf16[1024,256]{1,0:T(8,128)(2,1)}, bf16[1024,256]{1,0:T(8,128)(2,1)S(1)}, u32[]{:S(2)}, u32[]{:S(2)}) collective-permute-start(bf16[1024,256]{1,0:T(8,128)(2,1)} %param.9), channel_id=1, source_target_pairs={{0,1},{1,2},{2,3},{3,4},{4,5},{5,6},{6,7},{7,8},{8,9},{9,10},{10,1... | collective-permute-start | bytes 1572872 | tf_op jit(solution)/shard_map/ppermute | solution.py:15
  7.0 13.1 %collective-permute-start.1 = (bf16[1024,256]{1,0:T(8,128)(2,1)}, bf16[1024,256]{1,0:T(8,128)(2,1)S(1)}, u32[]{:S(2)}, u32[]{:S(2)}) collective-permute-start(bf16[1024,256]{1,0:T(8,128)(2,1)} %param.9), channel_id=1, source_target_pairs={{1,0},{2,1},{3,2},{4,3},{5,4},{6,5},{7,6},{8,7},{9,8},{10,9},{11,1... | collective-permute-start | bytes 1572872 | tf_op jit(solution)/shard_map/ppermute | solution.py:18
  57.5 12.4 %collective-permute-start.2 = (bf16[1024,256]{1,0:T(8,128)(2,1)S(1)}, bf16[1024,256]{1,0:T(8,128)(2,1)S(1)}, u32[]{:S(2)}, u32[]{:S(2)}) collective-permute-start(bf16[1024,256]{1,0:T(8,128)(2,1)S(1)} %bitcast.64), channel_id=1, source_target_pairs={{31,0},{0,1},{1,2},{2,3},{3,4},{4,5},{5,6},{6,7},{7,8},{8,9},{9,10... | collective-permute-start | bytes 1572872 | tf_op jit(solution)/shard_map/ppermute | solution.py:26
  61.6 8.3 %collective-permute-start.3 = (bf16[1024,256]{1,0:T(8,128)(2,1)S(1)}, bf16[1024,256]{1,0:T(8,128)(2,1)S(1)}, u32[]{:S(2)}, u32[]{:S(2)}) collective-permute-start(bf16[1024,256]{1,0:T(8,128)(2,1)S(1)} %bitcast.65), channel_id=1, source_target_pairs={{1,0},{2,1},{3,2},{4,3},{5,4},{6,5},{7,6},{8,7},{9,8},{10,9},{11,1... | collective-permute-start | bytes 1572872 | tf_op jit(solution)/shard_map/ppermute | solution.py:26
  70.0 1.0 copy-start.1
  209.4 0.7 copy-start.3
  245.8 2.0 copy-start.2
Sparse Core Ops, SparseCore 0:
  73.7 131.9 all-reduce.2
where the time goes:
time: 290 us; the launch traced here: 289 us
  waiting for transfers between devices  143 us (49%)
  other arithmetic  63.2 us (22%)
  local copies, waits for them, and re-layouts  29.3 us (10%)
  matrix products  26 us (9%)
  between operations  15.5 us (5%)
  starting transfers between devices  12 us (4%)
    psum x1, waiting for transfers between devices, on_device(): gram_matrix = lax.psum(local_gram, ('grp', 'row')) / rows_total  132 us
    another operation x6, other arithmetic, on_device(): factor_low = jnp.linalg.cholesky(gram_matrix)  34.2 us
    another operation x4, other arithmetic, on_device(): lax.linalg.triangular_solve(factor_low, local_y, left_side=False, lower=T...  22.5 us
    ppermute x2, waiting for transfers between devices, passed_along(): return lax.ppermute(block, axis, route)  6.15 us
    ppermute x1, starting transfers between devices, padded_2(): lax.ppermute(lax.slice_in_dim(block, 0, width, axis=dim), axis, backward)  5.91 us
  transfers between devices with their start and end apart: 5, of which 4 were waited for; matrix products, arithmetic and copies ran while one was open for 1% of the time, Pallas kernels for 0%

commit v1 on v0

v1 whole, which is shorter than its diff:
```python
import functools

import jax
import jax.numpy as jnp
from jax import lax
from jax.experimental import pallas as pl
from jax.experimental.pallas import tpu as pltpu
from jax.sharding import PartitionSpec as P

H = 2
BLOCK = 128
CHUNKS = 2
DIRECT_LIMIT = 32
MESH = pl.DeviceIdType.MESH
F32 = jnp.float32
BF16 = jnp.bfloat16
EXACT = lax.Precision.HIGHEST


def split_high_low(x):
    high = x.astype(BF16)
    return high, (x - high.astype(F32)).astype(BF16)


def dot(a, b, dims, precision=None):
    return lax.dot_general(
        a, b, (dims, ((), ())), precision=precision, preferred_element_type=F32
    )


NN = ((1,), (0,))
NT = ((1,), (1,))
TN = ((0,), (0,))


def dot_split(x, m, dims):
    xh, xl = split_high_low(x)
    mh, ml = split_high_low(m)
    return dot(xh, mh, dims) + (dot(xl, mh, dims) + dot(xh, ml, dims))


def on_ring(device, rows):
    return (device // rows, device % rows)


def step_kernel(
    direct, groups, rows, tile_total,
    row_ref, col_ref, count_ref, tiles_hbm, q_hbm,
    y_hbm, gram_ref,
    window, tiles, tiles_t, aq, send_lo, send_hi, recv_lo, recv_hi, y, acc, pair, shards,
    load_sems, q_sems, y_sems, pair_sems, rs_sems, ag_sems, out_sem,
):
    slots = tiles_hbm.shape[0]
    size = tiles_hbm.shape[1]
    own = q_hbm.shape[0] // size
    chunks = window.shape[0]
    width = window.shape[2]
    span = 2 * H + 1
    edge = H * size
    inner = own * size
    total = groups * rows
    g, r = lax.axis_index("grp"), lax.axis_index("row")
    me = g * rows + r
    nxt = on_ring((me + 1) % total, rows)
    prv = on_ring((me + total - 1) % total, rows)
    chips = total // 2
    parity = r % 2
    chip = me // 2
    mate = on_ring(chip * 2 + (1 - parity), rows)

    def peer(offset):
        return on_ring(((chip + offset) % chips) * 2 + parity, rows)

    loads = []
    for k in range(chunks):
        loads.append(pltpu.make_async_copy(
            q_hbm.at[:, pl.ds(k * width, width)],
            window.at[k, pl.ds(edge, inner)], load_sems.at[slots + k]))
        loads[-1].start()
    tile_loads = []
    for s in range(slots):
        tile_loads.append(pltpu.make_async_copy(tiles_hbm.at[s], tiles.at[s], load_sems.at[s]))
        tile_loads[-1].start()

    barrier = pltpu.get_barrier_semaphore()
    if direct:
        for other in range(1, total):
            pl.semaphore_signal(
                barrier, inc=1, device_id=on_ring((me + other) % total, rows),
                device_id_type=MESH)
        pl.semaphore_wait(barrier, total - 1)
    else:
        for other in (nxt, prv):
            pl.semaphore_signal(barrier, inc=1, device_id=other, device_id_type=MESH)
        pl.semaphore_wait(barrier, 2)

    def remote(src, dst, sems, index, device):
        return pltpu.make_async_remote_copy(
            src_ref=src, dst_ref=dst, send_sem=sems.at[0, index], recv_sem=sems.at[1, index],
            device_id=device, device_id_type=MESH)

    halo = []
    for k in range(chunks):
        loads[k].wait()
        up = remote(window.at[k, pl.ds(edge + inner - edge, edge)],
                    window.at[k, pl.ds(0, edge)], q_sems, 2 * k, nxt)
        down = remote(window.at[k, pl.ds(edge, edge)],
                      window.at[k, pl.ds(edge + inner, edge)], q_sems, 2 * k + 1, prv)
        up.start()
        down.start()
        halo.append((up, down))

    tiles[slots] = jnp.zeros((size, size), BF16)
    tiles_t[slots] = jnp.zeros((size, size), BF16)
    for s in range(slots):
        tile_loads[s].wait()
        tiles_t[s] = tiles[s].T

    slot_of = {}
    for row in range(own):
        for off in range(span):
            slot_of[row, off] = jnp.int32(slots)
    for s in range(slots):
        live = s < count_ref[0]
        at_row = row_ref[s] % own
        offset = (col_ref[s] - row_ref[s] + H + tile_total) % tile_total
        for row in range(own):
            for off in range(span):
                hit = live & (at_row == row) & (offset == off)
                slot_of[row, off] = jnp.where(hit, jnp.int32(s), slot_of[row, off])

    def terms(column):
        value = None
        for row in range(own):
            off = column - row
            if 0 <= off < span:
                part = dot(tiles_t[slot_of[row, off]], aq[row], NN)
                value = part if value is None else value + part
        return value

    rim = []
    for k in range(chunks):
        for copy in halo[k]:
            copy.wait_recv()
        for row in range(own):
            value = None
            for off in range(span):
                part = dot(tiles[slot_of[row, off]],
                           window[k, pl.ds((row + off) * size, size)], NN)
                value = part if value is None else value + part
            aq[row] = value.astype(BF16)
        for column in range(H):
            send_lo[k, pl.ds(column * size, size)] = terms(column).astype(BF16)
        down = remote(send_lo.at[k], recv_lo.at[k], y_sems, 2 * k, prv)
        down.start()
        for column in range(H):
            send_hi[k, pl.ds(column * size, size)] = terms(H + own + column).astype(BF16)
        up = remote(send_hi.at[k], recv_hi.at[k], y_sems, 2 * k + 1, nxt)
        up.start()
        rim.append((down, up))
        for column in range(own):
            y[k, pl.ds(column * size, size)] = terms(H + column)

    writes = []
    halves = []
    for k in range(chunks):
        rim[k][1].wait_recv()
        y[k, pl.ds(0, edge)] = y[k, pl.ds(0, edge)] + recv_hi[k].astype(F32)
        rim[k][0].wait_recv()
        y[k, pl.ds(inner - edge, edge)] = (
            y[k, pl.ds(inner - edge, edge)] + recv_lo[k].astype(F32))
        write = pltpu.make_async_copy(y.at[k], y_hbm.at[k], out_sem.at[k])
        write.start()
        writes.append(write)
        high, low = split_high_low(y[k])
        halves.append((high, low))
        for j in range(k + 1):
            jh, jl = halves[j]
            block = dot(jh, high, TN) + (dot(jh, low, TN) + dot(jl, high, TN))
            acc[k, pl.ds(j * width, width)] = block
            if j != k:
                acc[j, pl.ds(k * width, width)] = block.T

    if direct:
        rows_of = acc.shape[1] // chips
        trade = remote(acc.at[1 - parity], pair, pair_sems, 0, mate)
        trade.start()
        trade.wait()
        acc[parity] = acc[parity] + pair[...]
        scatter = []
        for o in range(1, chips):
            at = pl.multiple_of(((chip + o) % chips) * rows_of, rows_of)
            copy = remote(acc.at[parity, pl.ds(at, rows_of)], shards.at[o], rs_sems, o, peer(o))
            copy.start()
            scatter.append(copy)
        here = pl.multiple_of(chip * rows_of, rows_of)
        value = acc[parity, pl.ds(here, rows_of)]
        for o in range(1, chips):
            scatter[o - 1].wait_recv()
            value = value + shards[o]
        gram_ref[parity, pl.ds(here, rows_of)] = value
        gather = []
        for o in range(1, chips):
            copy = remote(gram_ref.at[parity, pl.ds(here, rows_of)],
                          gram_ref.at[parity, pl.ds(here, rows_of)], ag_sems, o, peer(o))
            copy.start()
            gather.append(copy)
        for o in range(1, chips):
            at = pl.multiple_of(((chip + chips - o) % chips) * rows_of, rows_of)
            remote(gram_ref.at[parity, pl.ds(here, rows_of)],
                   gram_ref.at[parity, pl.ds(at, rows_of)], ag_sems, o, peer(o)).wait_recv()
        back = remote(gram_ref.at[parity], gram_ref.at[parity], pair_sems, 1, mate)
        back.start()
        remote(gram_ref.at[parity], gram_ref.at[1 - parity], pair_sems, 1, mate).wait_recv()
        back.wait_send()
        for copy in scatter + gather:
            copy.wait_send()
    else:
        gram_ref[...] = acc[...]
    for k in range(chunks):
        for copy in halo[k] + rim[k]:
            copy.wait_send()
        writes[k].wait()


def inverse_factor(a):
    size = a.shape[0]
    groups = size // 8
    parts = [a[8 * i : 8 * i + 8] for i in range(groups)]
    lane = lax.broadcasted_iota(jnp.int32, (8, size), 1)
    sub = lax.broadcasted_iota(jnp.int32, (8, size), 0)
    pivots = [None] * groups
    for j in range(size):
        home, at = divmod(j, 8)
        columns = [
            jnp.broadcast_to(parts[i][:, j : j + 1], (8, size)) for i in range(home, groups)
        ]
        pivot = jnp.broadcast_to(columns[0][at : at + 1], (8, size))
        row = jnp.broadcast_to(parts[home][at : at + 1], (8, size))
        row = jnp.where(lane == j, 1.0, row) * (1.0 / pivot)
        prior = pivots[home]
        pivots[home] = pivot if prior is None else jnp.where(sub == at, pivot, prior)
        for i in range(home, groups):
            if i == home and at == 7:
                continue
            kept = jnp.where(lane == j, 0.0, parts[i])
            new = kept - columns[i - home] * row
            if i == home:
                new = jnp.where(sub > at, new, parts[i])
            parts[i] = new
    whole = []
    for i in range(groups):
        rows = sub + 8 * i
        unit = jnp.where(lane < rows, parts[i], jnp.where(lane == rows, 1.0, 0.0))
        whole.append(unit * lax.rsqrt(pivots[i]))
    return jnp.concatenate(whole, axis=0)


def solve_kernel(scale, y_hbm, gram_ref, out_hbm, y, out, in_sems, out_sems):
    blocks = y_hbm.shape[0]
    width = y_hbm.shape[2]
    reads = []
    for k in range(blocks):
        reads.append(pltpu.make_async_copy(y_hbm.at[k], y.at[k], in_sems.at[k]))
        reads[-1].start()
    gram = [
        [gram_ref[j, i * width : (i + 1) * width] * scale for j in range(blocks)]
        for i in range(blocks)
    ]
    for read in reads:
        read.wait()
    writes = []
    for k in range(blocks):
        inverse = inverse_factor(gram[k][k])
        basis = dot_split(y[k], inverse, NT)
        out[k] = basis
        write = pltpu.make_async_copy(
            out.at[k], out_hbm.at[:, pl.ds(k * width, width)], out_sems.at[k])
        write.start()
        writes.append(write)
        over = {j: dot(inverse, gram[k][j], NN, EXACT) for j in range(k + 1, blocks)}
        for i in range(k + 1, blocks):
            for j in range(i, blocks):
                gram[i][j] = gram[i][j] - dot(over[i], over[j], TN, EXACT)
            y[i] = y[i] - dot_split(basis, over[i], NN)
    for write in writes:
        write.wait()


def on_device(tiles, tile_row, tile_col, tile_count, q_block):
    slots, size, unused_size = tiles.shape
    height, basis = q_block.shape
    groups, rows = lax.axis_size("grp"), lax.axis_size("row")
    total = groups * rows
    own = height // size
    tile_total = own * total
    width = BLOCK
    chunks = basis // width
    edge = H * size
    direct = total <= DIRECT_LIMIT and (basis // (total // 2)) % 8 == 0
    chips = max(total // 2, 1)
    shard = basis // chips if direct else 8
    any_spec = pl.BlockSpec(memory_space=pl.ANY)
    vmem_spec = pl.BlockSpec(memory_space=pltpu.VMEM)
    smem_spec = pl.BlockSpec(memory_space=pltpu.SMEM)
    dma = pltpu.SemaphoreType.DMA
    y, gram = pl.pallas_call(
        functools.partial(step_kernel, direct, groups, rows, tile_total),
        out_shape=(
            jax.ShapeDtypeStruct((chunks, height, width), F32),
            jax.ShapeDtypeStruct((chunks, basis, width), F32),
        ),
        in_specs=[smem_spec, smem_spec, smem_spec, any_spec, any_spec],
        out_specs=(any_spec, vmem_spec),
        scratch_shapes=[
            pltpu.VMEM((chunks, height + 2 * edge, width), BF16),
            pltpu.VMEM((slots + 1, size, size), BF16),
            pltpu.VMEM((slots + 1, size, size), BF16),
            pltpu.VMEM((own, size, width), BF16),
            pltpu.VMEM((chunks, edge, width), BF16),
            pltpu.VMEM((chunks, edge, width), BF16),
            pltpu.VMEM((chunks, edge, width), BF16),
            pltpu.VMEM((chunks, edge, width), BF16),
            pltpu.VMEM((chunks, height, width), F32),
            pltpu.VMEM((chunks, basis, width), F32),
            pltpu.VMEM((basis, width), F32),
            pltpu.VMEM((chips if direct else 1, shard, width), F32),
            dma((slots + chunks,)),
            dma((2, 2 * chunks)),
            dma((2, 2 * chunks)),
            dma((2, 2)),
            dma((2, chips if direct else 1)),
            dma((2, chips if direct else 1)),
            dma((chunks,)),
        ],
        compiler_params=pltpu.CompilerParams(
            collective_id=0, has_side_effects=True, vmem_limit_bytes=40 * 2**20
        ),
    )(tile_row, tile_col, tile_count, tiles, q_block)
    if not direct:
        gram = lax.psum(gram, ("grp", "row"))
    return pl.pallas_call(
        functools.partial(solve_kernel, 1.0 / (height * total)),
        out_shape=jax.ShapeDtypeStruct((height, basis), F32),
        in_specs=[any_spec, vmem_spec],
        out_specs=any_spec,
        scratch_shapes=[
            pltpu.VMEM((chunks, height, width), F32),
            pltpu.VMEM((chunks, height, width), F32),
            dma((chunks,)),
            dma((chunks,)),
        ],
        compiler_params=pltpu.CompilerParams(vmem_limit_bytes=40 * 2**20),
    )(y, gram)


def solution(mesh):
    placed = (
        P(("grp", "row"), None, None),
        P(("grp", "row")),
        P(("grp", "row")),
        P(("grp", "row")),
        P(("grp", "row"), None),
    )
    return jax.shard_map(
        on_device, mesh=mesh, in_specs=placed, out_specs=P(("grp", "row"), None), check_vma=False
    )
```

time: 290 us -> 89.5 us (0.31)
  waiting for transfers between devices: 143 us -> 0 us
  Pallas kernels: 0 us -> 84.2 us
  other arithmetic: 63.2 us -> 0 us
  matrix products: 26 us -> 0 us
  local copies, waits for them, and re-layouts: 29.3 us -> 4.23 us
  between operations: 15.5 us -> 0.83 us
  starting transfers between devices: 12 us -> 0 us
    psum x1 -> x0, waiting for transfers between devices: 132 us -> none  [on_device(): gram_matrix = lax.psum(local_gram, ('grp', 'row')) / rows_total]
    pallas_call x0 -> x2, Pallas kernels: none -> 84.2 us  [the longest x1 47.8 us: on_device(): pl.pallas_call(functools.partial(step_kernel, direct, groups, rows, tile_...]
    another operation x10 -> x0, other arithmetic: 56.7 us -> none  [the longest x6 34.2 us: on_device(): factor_low = jnp.linalg.cholesky(gram_matrix)]
    dot_general x5 -> x0, matrix products: 19.5 us -> none  [the longest x1 4.3 us: on_device(): jnp.einsum('rs,sak->rak', row_place, products, precision=lax.Precision.HI...]
    ppermute x4 -> x0, starting transfers between devices: 12 us -> none  [the longest x1 5.91 us: padded_2(): lax.ppermute(lax.slice_in_dim(block, 0, width, axis=dim), axis, backward)]
    ppermute x4 -> x0, waiting for transfers between devices: 11.3 us -> none  [the longest x2 6.15 us: passed_along(): return lax.ppermute(block, axis, route)]
    dot_general x2 -> x0, local copies, waits for them, and re-layouts: 10.2 us -> none  [the longest x1 5.11 us: on_device(): jnp.einsum('sab,sbk->sak', tiles, blocks, preferred_element_type=jnp.floa...]
    another operation x10 -> x0, local copies, waits for them, and re-layouts: 7.9 us -> none
  transfers between devices with their start and end apart: 5 -> 0, of which waited for: 4 -> 0; matrix products, arithmetic and copies ran while one was open for 1% -> 0% of each run, Pallas kernels for 0% -> 0%
where the time goes in v1:
time: 89.5 us; the launch traced here: 89.3 us
  Pallas kernels  84.2 us (94%)
  local copies, waits for them, and re-layouts  4.23 us (5%)
    pallas_call x1, Pallas kernels, on_device(): pl.pallas_call(functools.partial(step_kernel, direct, groups, rows, tile_...  47.8 us
    pallas_call x1, Pallas kernels, on_device(): pl.pallas_call(functools.partial(solve_kernel, 1.0 / (height * total)), o...  36.4 us
    unnamed x8, local copies, waits for them, and re-layouts  4.23 us

profile of v1, /device:TPU:0, one launch (start us, length us, event | category | flops | bytes accessed | tf_op | source)
XLA Modules:
  0.0 89.3 jit_solution(5598349639762222637)
XLA Ops:
  0.7 0.0 copy-start
  0.7 1.9 %copy-done = bf16[6,512,512]{2,1,0:T(8,128)(2,1)S(1)} copy-done((bf16[6,512,512]{2,1,0:T(8,128)(2,1)S(1)}, bf16[6,512,512]{2,1,0:T(8,128)(2,1)}, u32[]{:S(2)}) %copy-start) | copy-done | bytes 3145752
  2.5 0.0 copy-start.1
  2.5 1.0 %copy-done.1 = bf16[1024,256]{1,0:T(8,128)(2,1)S(1)} copy-done((bf16[1024,256]{1,0:T(8,128)(2,1)S(1)}, bf16[1024,256]{1,0:T(8,128)(2,1)}, u32[]{:S(2)}) %copy-start.1) | copy-done | bytes 524312
  3.6 0.0 copy-start.2
  3.6 0.7 copy-done.2
  4.2 0.0 copy-start.3
  4.2 0.7 copy-done.3
  4.9 47.8 %shard_map.55 = (f32[2,1024,128]{2,1,0:T(8,128)S(1)}, f32[2,256,128]{2,1,0:T(8,128)S(1)}) custom-call(s32[6]{0:T(128)S(1)} %copy-done.2, s32[6]{0:T(128)S(1)} %copy-done.3, s32[1]{0:T(128)S(6)} %copy.6.count_ref, bf16[6,512,512]{2,1,0:T(8,128)(2,1)S(1)} %copy-done, bf16[1024,256]{1,0:T(8,128)(2,1)S(1)} %copy-done.1), custom_call_target="tpu_custom_call" | custom-call | tf_op jit(solution)/shard_map/pallas_call | solution.py:307
  52.7 36.4 %shard_map.56 = f32[1024,256]{1,0:T(8,128)} custom-call(f32[2,1024,128]{2,1,0:T(8,128)S(1)} %get-tuple-element.7.y_hbm, f32[2,256,128]{2,1,0:T(8,128)S(1)} %get-tuple-element.8.gram_ref), custom_call_target="tpu_custom_call" | custom-call | tf_op jit(solution)/shard_map/pallas_call | solution.py:342
Async XLA Ops:
  0.7 1.9 %copy-start = (bf16[6,512,512]{2,1,0:T(8,128)(2,1)S(1)}, bf16[6,512,512]{2,1,0:T(8,128)(2,1)}, u32[]{:S(2)}) copy-start(bf16[6,512,512]{2,1,0:T(8,128)(2,1)} %tiles_hbm.1) | copy-start | bytes 9437188
  2.5 1.0 %copy-start.1 = (bf16[1024,256]{1,0:T(8,128)(2,1)S(1)}, bf16[1024,256]{1,0:T(8,128)(2,1)}, u32[]{:S(2)}) copy-start(bf16[1024,256]{1,0:T(8,128)(2,1)} %q_hbm.1) | copy-start | bytes 1572868
  3.6 0.7 copy-start.2
  4.2 0.7 copy-start.3

commit v2 on v1

--- a/solution.py
+++ b/solution.py
@@ -11,6 +11,7 @@
 BLOCK = 128
 CHUNKS = 2
 DIRECT_LIMIT = 32
+VMEM_LIMIT = 67_043_328
 MESH = pl.DeviceIdType.MESH
 F32 = jnp.float32
 BF16 = jnp.bfloat16
@@ -45,10 +46,10 @@
 
 def step_kernel(
     direct, groups, rows, tile_total,
-    row_ref, col_ref, count_ref, tiles_hbm, q_hbm,
+    row_hbm, col_hbm, count_hbm, tiles_hbm, q_hbm,
     y_hbm, gram_ref,
-    window, tiles, tiles_t, aq, send_lo, send_hi, recv_lo, recv_hi, y, acc, pair, shards,
-    load_sems, q_sems, y_sems, pair_sems, rs_sems, ag_sems, out_sem,
+    row_ref, col_ref, count_ref, window, tiles, tiles_t, aq, send_lo, send_hi, recv_lo, recv_hi, y, acc, pair, shards,
+    load_sems, q_sems, y_sems, pair_sems, rs_sems, ag_sems, out_sem, index_sems,
 ):
     slots = tiles_hbm.shape[0]
     size = tiles_hbm.shape[1]
@@ -82,6 +83,13 @@
         tile_loads.append(pltpu.make_async_copy(tiles_hbm.at[s], tiles.at[s], load_sems.at[s]))
         tile_loads[-1].start()
 
+    index_loads = []
+    for k, (src, dst) in enumerate(
+        ((row_hbm, row_ref), (col_hbm, col_ref), (count_hbm, count_ref))
+    ):
+        index_loads.append(pltpu.make_async_copy(src, dst, index_sems.at[k]))
+        index_loads[-1].start()
+
     barrier = pltpu.get_barrier_semaphore()
     if direct:
         for other in range(1, total):
@@ -116,6 +124,8 @@
         tile_loads[s].wait()
         tiles_t[s] = tiles[s].T
 
+    for load in index_loads:
+        load.wait()
     slot_of = {}
     for row in range(own):
         for off in range(span):
@@ -229,30 +239,43 @@
     parts = [a[8 * i : 8 * i + 8] for i in range(groups)]
     lane = lax.broadcasted_iota(jnp.int32, (8, size), 1)
     sub = lax.broadcasted_iota(jnp.int32, (8, size), 0)
-    pivots = [None] * groups
-    for j in range(size):
-        home, at = divmod(j, 8)
+
+    def row_of(x, at):
+        return jnp.broadcast_to(x[at : at + 1], (8, size))
+
+    whole = []
+    for home in range(groups):
+        first = 8 * home
+        later = range(home, groups)
         columns = [
-            jnp.broadcast_to(parts[i][:, j : j + 1], (8, size)) for i in range(home, groups)
+            {i: jnp.broadcast_to(parts[i][:, first + l : first + l + 1], (8, size)) for i in later}
+            for l in range(8)
         ]
-        pivot = jnp.broadcast_to(columns[0][at : at + 1], (8, size))
-        row = jnp.broadcast_to(parts[home][at : at + 1], (8, size))
-        row = jnp.where(lane == j, 1.0, row) * (1.0 / pivot)
-        prior = pivots[home]
-        pivots[home] = pivot if prior is None else jnp.where(sub == at, pivot, prior)
-        for i in range(home, groups):
-            if i == home and at == 7:
-                continue
-            kept = jnp.where(lane == j, 0.0, parts[i])
-            new = kept - columns[i - home] * row
-            if i == home:
-                new = jnp.where(sub > at, new, parts[i])
-            parts[i] = new
-    whole = []
-    for i in range(groups):
-        rows = sub + 8 * i
-        unit = jnp.where(lane < rows, parts[i], jnp.where(lane == rows, 1.0, 0.0))
-        whole.append(unit * lax.rsqrt(pivots[i]))
+        mine = parts[home]
+        rows = []
+        pivots = None
+        for j in range(8):
+            top = columns[j][home]
+            pivot = row_of(top, j)
+            inv = 1.0 / pivot
+            pivots = pivot if pivots is None else jnp.where(sub == j, pivot, pivots)
+            row = jnp.where(lane == first + j, 1.0, row_of(mine, j)) * inv
+            rows.append(jnp.where((lane > first + j) & (lane < first + 8), 0.0, row))
+            mine = jnp.where(
+                sub > j, jnp.where(lane == first + j, 0.0, mine) - top * row, mine)
+            for l in range(j + 1, 8):
+                weight = row_of(top, l) * inv
+                for i in later:
+                    columns[l][i] = columns[l][i] - columns[j][i] * weight
+        for i in later:
+            if i > home:
+                value = jnp.where((lane >= first) & (lane < first + 8), 0.0, parts[i])
+                for j in range(8):
+                    value = value - columns[j][i] * rows[j]
+                parts[i] = value
+        at = sub + first
+        unit = jnp.where(lane < at, mine, jnp.where(lane == at, 1.0, 0.0))
+        whole.append(unit * lax.rsqrt(pivots))
     return jnp.concatenate(whole, axis=0)
 
 
@@ -302,7 +325,7 @@
     shard = basis // chips if direct else 8
     any_spec = pl.BlockSpec(memory_space=pl.ANY)
     vmem_spec = pl.BlockSpec(memory_space=pltpu.VMEM)
-    smem_spec = pl.BlockSpec(memory_space=pltpu.SMEM)
+    hbm_spec = pl.BlockSpec(memory_space=pltpu.HBM)
     dma = pltpu.SemaphoreType.DMA
     y, gram = pl.pallas_call(
         functools.partial(step_kernel, direct, groups, rows, tile_total),
@@ -310,9 +333,12 @@
             jax.ShapeDtypeStruct((chunks, height, width), F32),
             jax.ShapeDtypeStruct((chunks, basis, width), F32),
         ),
-        in_specs=[smem_spec, smem_spec, smem_spec, any_spec, any_spec],
+        in_specs=[hbm_spec] * 5,
         out_specs=(any_spec, vmem_spec),
         scratch_shapes=[
+            pltpu.SMEM(tile_row.shape, jnp.int32),
+            pltpu.SMEM(tile_col.shape, jnp.int32),
+            pltpu.SMEM(tile_count.shape, jnp.int32),
             pltpu.VMEM((chunks, height + 2 * edge, width), BF16),
             pltpu.VMEM((slots + 1, size, size), BF16),
             pltpu.VMEM((slots + 1, size, size), BF16),
@@ -332,9 +358,10 @@
             dma((2, chips if direct else 1)),
             dma((2, chips if direct else 1)),
             dma((chunks,)),
+            dma((3,)),
         ],
         compiler_params=pltpu.CompilerParams(
-            collective_id=0, has_side_effects=True, vmem_limit_bytes=40 * 2**20
+            collective_id=0, has_side_effects=True, vmem_limit_bytes=VMEM_LIMIT
         ),
     )(tile_row, tile_col, tile_count, tiles, q_block)
     if not direct:
@@ -350,7 +377,7 @@
             dma((chunks,)),
             dma((chunks,)),
         ],
-        compiler_params=pltpu.CompilerParams(vmem_limit_bytes=40 * 2**20),
+        compiler_params=pltpu.CompilerParams(vmem_limit_bytes=VMEM_LIMIT),
     )(y, gram)
 
 

time: 89.5 us -> 60.8 us (0.68)
  Pallas kernels: 84.2 us -> 60 us
  local copies, waits for them, and re-layouts: 4.23 us -> 0 us
    pallas_call x1, Pallas kernels: 36.4 us -> 12.3 us  [on_device(): pl.pallas_call(functools.partial(solve_kernel, 1.0 / (height * total)), o...]
    unnamed x8 -> x0, local copies, waits for them, and re-layouts: 4.23 us -> none
where the time goes in v2:
time: 60.8 us; the launch traced here: 60.6 us
  Pallas kernels  60 us (99%)
  between operations  0.66 us (1%)
    pallas_call x1, Pallas kernels, on_device(): pl.pallas_call(functools.partial(step_kernel, direct, groups, rows, tile_...  47.7 us
    pallas_call x1, Pallas kernels, on_device(): pl.pallas_call(functools.partial(solve_kernel, 1.0 / (height * total)), o...  12.3 us

profile of v2, /device:TPU:0, one launch (start us, length us, event | category | flops | bytes accessed | tf_op | source)
XLA Modules:
  0.0 60.6 jit_solution(15563205912048492988)
XLA Ops:
  0.7 47.7 %shard_map.55 = (f32[2,1024,128]{2,1,0:T(8,128)}, f32[2,256,128]{2,1,0:T(8,128)}) custom-call(s32[6]{0:T(128)} %row_hbm.1, s32[6]{0:T(128)} %col_hbm.1, s32[1]{0:T(128)S(6)} %copy.6.count_hbm, bf16[6,512,512]{2,1,0:T(8,128)(2,1)} %tiles_hbm.1, bf16[1024,256]{1,0:T(8,128)(2,1)} %q_hbm.1), custom_call_target="tpu_custom_call" | custom-call | tf_op jit(solution)/shard_map/pallas_call | solution.py:330
  48.4 12.3 %shard_map.56 = f32[1024,256]{1,0:T(8,128)} custom-call(f32[2,1024,128]{2,1,0:T(8,128)} %get-tuple-element.7.y_hbm, f32[2,256,128]{2,1,0:T(8,128)} %get-tuple-element.8.gram_ref), custom_call_target="tpu_custom_call" | custom-call | tf_op jit(solution)/shard_map/pallas_call | solution.py:369

commit v3 on v2

--- a/solution.py
+++ b/solution.py
@@ -45,11 +45,11 @@
 
 
 def step_kernel(
-    direct, groups, rows, tile_total,
+    direct, scale, groups, rows, tile_total,
     row_hbm, col_hbm, count_hbm, tiles_hbm, q_hbm,
-    y_hbm, gram_ref,
+    y_hbm, gram_ref, inverse_ref,
     row_ref, col_ref, count_ref, window, tiles, tiles_t, aq, send_lo, send_hi, recv_lo, recv_hi, y, acc, pair, shards,
-    load_sems, q_sems, y_sems, pair_sems, rs_sems, ag_sems, out_sem, index_sems,
+    acc_first, gram_first, shards_first, swap, load_sems, q_sems, y_sems, pair_sems, rs_sems, ag_sems, rs_first, ag_first, out_sem, index_sems,
 ):
     slots = tiles_hbm.shape[0]
     size = tiles_hbm.shape[1]
@@ -106,6 +106,41 @@
         return pltpu.make_async_remote_copy(
             src_ref=src, dst_ref=dst, send_sem=sems.at[0, index], recv_sem=sems.at[1, index],
             device_id=device, device_id_type=MESH)
+
+    if direct:
+        rows_of = width // chips
+        here = pl.multiple_of(chip * rows_of, rows_of)
+
+    def scatter(source, landing, sems):
+        copies = []
+        for o in range(1, chips):
+            at = pl.multiple_of(((chip + o) % chips) * rows_of, rows_of)
+            copies.append(
+                remote(source.at[pl.ds(at, rows_of)], landing.at[o], sems, o, peer(o)))
+            copies[-1].start()
+        return copies
+
+    def collect(copies, source, landing):
+        value = source[pl.ds(here, rows_of)]
+        for o in range(1, chips):
+            copies[o - 1].wait_recv()
+            value = value + landing[o]
+        return value
+
+    def gather(target, sems):
+        copies = []
+        for o in range(1, chips):
+            copies.append(remote(
+                target.at[pl.ds(here, rows_of)], target.at[pl.ds(here, rows_of)],
+                sems, o, peer(o)))
+            copies[-1].start()
+        return copies
+
+    def gathered(target, sems):
+        for o in range(1, chips):
+            at = pl.multiple_of(((chip + chips - o) % chips) * rows_of, rows_of)
+            remote(target.at[pl.ds(here, rows_of)], target.at[pl.ds(at, rows_of)],
+                   sems, o, peer(o)).wait_recv()
 
     halo = []
     for k in range(chunks):
@@ -187,45 +222,42 @@
         for j in range(k + 1):
             jh, jl = halves[j]
             block = dot(jh, high, TN) + (dot(jh, low, TN) + dot(jl, high, TN))
-            acc[k, pl.ds(j * width, width)] = block
-            if j != k:
-                acc[j, pl.ds(k * width, width)] = block.T
+            if not direct:
+                acc[k, pl.ds(j * width, width)] = block
+                if j != k:
+                    acc[j, pl.ds(k * width, width)] = block.T
+            elif k == 0:
+                acc_first[...] = block
+            else:
+                acc[j] = block
+        if direct and k == 0:
+            scatter_first = scatter(acc_first, shards_first, rs_first)
 
     if direct:
-        rows_of = acc.shape[1] // chips
         trade = remote(acc.at[1 - parity], pair, pair_sems, 0, mate)
         trade.start()
+        swap[0] = collect(scatter_first, acc_first, shards_first)
+        swapped = remote(swap.at[0], swap.at[1], pair_sems, 2, mate)
+        swapped.start()
         trade.wait()
         acc[parity] = acc[parity] + pair[...]
-        scatter = []
-        for o in range(1, chips):
-            at = pl.multiple_of(((chip + o) % chips) * rows_of, rows_of)
-            copy = remote(acc.at[parity, pl.ds(at, rows_of)], shards.at[o], rs_sems, o, peer(o))
-            copy.start()
-            scatter.append(copy)
-        here = pl.multiple_of(chip * rows_of, rows_of)
-        value = acc[parity, pl.ds(here, rows_of)]
-        for o in range(1, chips):
-            scatter[o - 1].wait_recv()
-            value = value + shards[o]
-        gram_ref[parity, pl.ds(here, rows_of)] = value
-        gather = []
-        for o in range(1, chips):
-            copy = remote(gram_ref.at[parity, pl.ds(here, rows_of)],
-                          gram_ref.at[parity, pl.ds(here, rows_of)], ag_sems, o, peer(o))
-            copy.start()
-            gather.append(copy)
-        for o in range(1, chips):
-            at = pl.multiple_of(((chip + chips - o) % chips) * rows_of, rows_of)
-            remote(gram_ref.at[parity, pl.ds(here, rows_of)],
-                   gram_ref.at[parity, pl.ds(at, rows_of)], ag_sems, o, peer(o)).wait_recv()
+        scatter_rest = scatter(acc.at[parity], shards, rs_sems)
+        swapped.wait()
+        gram_first[pl.ds(here, rows_of)] = swap[0] + swap[1]
+        gather_first = gather(gram_first, ag_first)
+        gram_ref[parity, pl.ds(here, rows_of)] = collect(scatter_rest, acc.at[parity], shards)
+        gather_rest = gather(gram_ref.at[parity], ag_sems)
+        gathered(gram_first, ag_first)
+        inverse_ref[...] = inverse_factor(gram_first[...] * scale)
+        gathered(gram_ref.at[parity], ag_sems)
         back = remote(gram_ref.at[parity], gram_ref.at[parity], pair_sems, 1, mate)
         back.start()
         remote(gram_ref.at[parity], gram_ref.at[1 - parity], pair_sems, 1, mate).wait_recv()
         back.wait_send()
-        for copy in scatter + gather:
+        for copy in scatter_first + gather_first + scatter_rest + gather_rest:
             copy.wait_send()
     else:
+        inverse_ref[...] = jnp.zeros_like(inverse_ref)
         gram_ref[...] = acc[...]
     for k in range(chunks):
         for copy in halo[k] + rim[k]:
@@ -310,6 +342,33 @@
         write.wait()
 
 
+def finish_kernel(scale, y_hbm, gram_ref, inverse_ref, out_hbm, y, out, in_sems, out_sems):
+    width = y_hbm.shape[2]
+
+    def read(k):
+        return pltpu.make_async_copy(y_hbm.at[k], y.at[k], in_sems.at[k])
+
+    def write(k):
+        return pltpu.make_async_copy(
+            out.at[k], out_hbm.at[:, pl.ds(k * width, width)], out_sems.at[k])
+
+    for k in range(2):
+        read(k).start()
+    first = inverse_ref[...]
+    over = dot(first, gram_ref[0] * scale, NN, EXACT)
+    rest = gram_ref[1] * scale - dot(over, over, TN, EXACT)
+    read(0).wait()
+    basis = dot_split(y[0], first, NT)
+    out[0] = basis
+    write(0).start()
+    read(1).wait()
+    y[1] = y[1] - dot_split(basis, over, NN)
+    out[1] = dot_split(y[1], inverse_factor(rest), NT)
+    write(1).start()
+    for k in range(2):
+        write(k).wait()
+
+
 def on_device(tiles, tile_row, tile_col, tile_count, q_block):
     slots, size, unused_size = tiles.shape
     height, basis = q_block.shape
@@ -320,21 +379,27 @@
     width = BLOCK
     chunks = basis // width
     edge = H * size
-    direct = total <= DIRECT_LIMIT and (basis // (total // 2)) % 8 == 0
     chips = max(total // 2, 1)
-    shard = basis // chips if direct else 8
+    direct = (
+        total <= DIRECT_LIMIT and rows % 2 == 0 and chunks == 2 and width % (8 * chips) == 0
+    )
+    shard = width // chips if direct else 8
+    partners = chips if direct else 1
+    reduced = (chunks, width if direct else basis, width)
+    scale = 1.0 / (height * total)
     any_spec = pl.BlockSpec(memory_space=pl.ANY)
     vmem_spec = pl.BlockSpec(memory_space=pltpu.VMEM)
     hbm_spec = pl.BlockSpec(memory_space=pltpu.HBM)
     dma = pltpu.SemaphoreType.DMA
-    y, gram = pl.pallas_call(
-        functools.partial(step_kernel, direct, groups, rows, tile_total),
+    y, gram, inverse = pl.pallas_call(
+        functools.partial(step_kernel, direct, scale, groups, rows, tile_total),
         out_shape=(
             jax.ShapeDtypeStruct((chunks, height, width), F32),
-            jax.ShapeDtypeStruct((chunks, basis, width), F32),
+            jax.ShapeDtypeStruct(reduced, F32),
+            jax.ShapeDtypeStruct((width, width), F32),
         ),
         in_specs=[hbm_spec] * 5,
-        out_specs=(any_spec, vmem_spec),
+        out_specs=(any_spec, vmem_spec, vmem_spec),
         scratch_shapes=[
             pltpu.SMEM(tile_row.shape, jnp.int32),
             pltpu.SMEM(tile_col.shape, jnp.int32),
@@ -348,15 +413,21 @@
             pltpu.VMEM((chunks, edge, width), BF16),
             pltpu.VMEM((chunks, edge, width), BF16),
             pltpu.VMEM((chunks, height, width), F32),
-            pltpu.VMEM((chunks, basis, width), F32),
-            pltpu.VMEM((basis, width), F32),
-            pltpu.VMEM((chips if direct else 1, shard, width), F32),
+            pltpu.VMEM(reduced, F32),
+            pltpu.VMEM(reduced[1:], F32),
+            pltpu.VMEM((partners, shard, width), F32),
+            pltpu.VMEM((width, width), F32),
+            pltpu.VMEM((width, width), F32),
+            pltpu.VMEM((partners, shard, width), F32),
+            pltpu.VMEM((2, shard, width), F32),
             dma((slots + chunks,)),
             dma((2, 2 * chunks)),
             dma((2, 2 * chunks)),
-            dma((2, 2)),
-            dma((2, chips if direct else 1)),
-            dma((2, chips if direct else 1)),
+            dma((2, 3)),
+            dma((2, partners)),
+            dma((2, partners)),
+            dma((2, partners)),
+            dma((2, partners)),
             dma((chunks,)),
             dma((3,)),
         ],
@@ -366,10 +437,12 @@
     )(tile_row, tile_col, tile_count, tiles, q_block)
     if not direct:
         gram = lax.psum(gram, ("grp", "row"))
+    last = finish_kernel if direct else solve_kernel
+    operands = (y, gram, inverse) if direct else (y, gram)
     return pl.pallas_call(
-        functools.partial(solve_kernel, 1.0 / (height * total)),
+        functools.partial(last, scale),
         out_shape=jax.ShapeDtypeStruct((height, basis), F32),
-        in_specs=[any_spec, vmem_spec],
+        in_specs=[any_spec] + [vmem_spec] * (len(operands) - 1),
         out_specs=any_spec,
         scratch_shapes=[
             pltpu.VMEM((chunks, height, width), F32),
@@ -378,7 +451,7 @@
             dma((chunks,)),
         ],
         compiler_params=pltpu.CompilerParams(vmem_limit_bytes=VMEM_LIMIT),
-    )(y, gram)
+    )(*operands)
 
 
 def solution(mesh):

time: 60.8 us -> 57.4 us (0.944)
  Pallas kernels: 60 us -> 56.4 us
    pallas_call x2, Pallas kernels: 60 us -> 56.4 us  [the longest x1 48.1 us: on_device(): pl.pallas_call(functools.partial(step_kernel, direct, scale, groups, rows...]
where the time goes in v3:
time: 57.4 us; the launch traced here: 57.2 us
  Pallas kernels  56.4 us (98%)
  between operations  0.82 us (1%)
    pallas_call x1, Pallas kernels, on_device(): pl.pallas_call(functools.partial(step_kernel, direct, scale, groups, rows...  48.1 us
    pallas_call x1, Pallas kernels, on_device(): pl.pallas_call(functools.partial(last, scale), out_shape=jax.ShapeDtypeSt...  8.26 us

profile of v3, /device:TPU:0, one launch (start us, length us, event | category | flops | bytes accessed | tf_op | source)
XLA Modules:
  0.0 57.2 jit_solution(856558375407469398)
XLA Ops:
  0.7 48.1 %shard_map.55 = (f32[2,1024,128]{2,1,0:T(8,128)}, f32[2,128,128]{2,1,0:T(8,128)}, f32[128,128]{1,0:T(8,128)}) custom-call(s32[6]{0:T(128)} %row_hbm.1, s32[6]{0:T(128)} %col_hbm.1, s32[1]{0:T(128)S(6)} %copy.6.count_hbm, bf16[6,512,512]{2,1,0:T(8,128)(2,1)} %tiles_hbm.1, bf16[1024,256]{1,0:T(8,128)(2,1)} %q_hbm.1), custom_call_target="tpu_custom_call" | custom-call | tf_op jit(solution)/shard_map/pallas_call | solution.py:394
  48.8 8.3 %shard_map.56 = f32[1024,256]{1,0:T(8,128)} custom-call(f32[2,1024,128]{2,1,0:T(8,128)} %get-tuple-element.8.y_hbm, f32[2,128,128]{2,1,0:T(8,128)} %get-tuple-element.9.gram_ref, f32[128,128]{1,0:T(8,128)} %get-tuple-element.10.inverse_ref), custom_call_target="tpu_custom_call" | custom-call | tf_op jit(solution)/shard_map/pallas_call | solution.py:442

commit v4 on v3

--- a/solution.py
+++ b/solution.py
@@ -49,7 +49,7 @@
     row_hbm, col_hbm, count_hbm, tiles_hbm, q_hbm,
     y_hbm, gram_ref, inverse_ref,
     row_ref, col_ref, count_ref, window, tiles, tiles_t, aq, send_lo, send_hi, recv_lo, recv_hi, y, acc, pair, shards,
-    acc_first, gram_first, shards_first, swap, load_sems, q_sems, y_sems, pair_sems, rs_sems, ag_sems, rs_first, ag_first, out_sem, index_sems,
+    acc_first, gram_first, shards_first, swap, kept, load_sems, q_sems, y_sems, pair_sems, rs_sems, ag_sems, rs_first, ag_first, out_sem, index_sems,
 ):
     slots = tiles_hbm.shape[0]
     size = tiles_hbm.shape[1]
@@ -218,10 +218,14 @@
         write.start()
         writes.append(write)
         high, low = split_high_low(y[k])
-        halves.append((high, low))
+        high_t = high.T
+        cross = dot(high_t, low, NN)
         for j in range(k + 1):
-            jh, jl = halves[j]
-            block = dot(jh, high, TN) + (dot(jh, low, TN) + dot(jl, high, TN))
+            if j == k:
+                block = dot(high_t, high, NN) + (cross + cross.T)
+            else:
+                block = dot(halves[j][0][...], high, NN) + (
+                    dot(halves[j][0][...], low, NN) + dot(halves[j][1][...], high, NN))
             if not direct:
                 acc[k, pl.ds(j * width, width)] = block
                 if j != k:
@@ -232,6 +236,10 @@
                 acc[j] = block
         if direct and k == 0:
             scatter_first = scatter(acc_first, shards_first, rs_first)
+        if k + 1 < chunks:
+            kept[2 * k] = high_t
+            kept[2 * k + 1] = low.T
+            halves.append((kept.at[2 * k], kept.at[2 * k + 1]))
 
     if direct:
         trade = remote(acc.at[1 - parity], pair, pair_sems, 0, mate)
@@ -420,6 +428,7 @@
             pltpu.VMEM((width, width), F32),
             pltpu.VMEM((partners, shard, width), F32),
             pltpu.VMEM((2, shard, width), F32),
+            pltpu.VMEM((2 * chunks, width, height), BF16),
             dma((slots + chunks,)),
             dma((2, 2 * chunks)),
             dma((2, 2 * chunks)),

time: 57.4 us -> 57.3 us (level)
  no operation moved by 1% of the time
where the time goes in v4:
time: 57.3 us; the launch traced here: 57.2 us
  Pallas kernels  56.4 us (98%)
  between operations  0.82 us (1%)
    pallas_call x1, Pallas kernels, on_device(): pl.pallas_call(functools.partial(step_kernel, direct, scale, groups, rows...  48.1 us
    pallas_call x1, Pallas kernels, on_device(): pl.pallas_call(functools.partial(last, scale), out_shape=jax.ShapeDtypeSt...  8.26 us

profile of v4, /device:TPU:0, one launch (start us, length us, event | category | flops | bytes accessed | tf_op | source)
XLA Modules:
  0.0 57.2 jit_solution(13945716796278237089)
XLA Ops:
  0.7 48.1 %shard_map.55 = (f32[2,1024,128]{2,1,0:T(8,128)}, f32[2,128,128]{2,1,0:T(8,128)}, f32[128,128]{1,0:T(8,128)}) custom-call(s32[6]{0:T(128)} %row_hbm.1, s32[6]{0:T(128)} %col_hbm.1, s32[1]{0:T(128)S(6)} %copy.6.count_hbm, bf16[6,512,512]{2,1,0:T(8,128)(2,1)} %tiles_hbm.1, bf16[1024,256]{1,0:T(8,128)(2,1)} %q_hbm.1), custom_call_target="tpu_custom_call" | custom-call | tf_op jit(solution)/shard_map/pallas_call | solution.py:402
  48.8 8.3 %shard_map.56 = f32[1024,256]{1,0:T(8,128)} custom-call(f32[2,1024,128]{2,1,0:T(8,128)} %get-tuple-element.8.y_hbm, f32[2,128,128]{2,1,0:T(8,128)} %get-tuple-element.9.gram_ref, f32[128,128]{1,0:T(8,128)} %get-tuple-element.10.inverse_ref), custom_call_target="tpu_custom_call" | custom-call | tf_op jit(solution)/shard_map/pallas_call | solution.py:451
